TPU v7x, 256 devices: a whole 4x4x8 slice. The times are simulated.
256 devices in a mesh: shard: 64 (over z, x, core), width: 4 (over y).
Axes of the slice: x: 4, y: 4, z: 8, core: 2. Of those that a mesh axis runs over, the one named last changes fastest.
Arguments:
- w_query: float32 [4096, 4096], P('shard', 'width'), may hold values from -0.25 to 0.25
- first_query: float32 [4096, 4096], P('shard', 'width'), may hold values from -0.09375 to 0.09375
- second_query: float32 [4096, 4096], P('shard', 'width'), may hold values from -0.09375 to 0.09375
- w_key: float32 [4096, 1024], P('shard', 'width'), may hold values from -0.25 to 0.25
- first_key: float32 [4096, 1024], P('shard', 'width'), may hold values from -0.09375 to 0.09375
- second_key: float32 [4096, 1024], P('shard', 'width'), may hold values from -0.09375 to 0.09375
- w_value: float32 [4096, 1024], P('shard', 'width'), may hold values from -0.25 to 0.25
- first_value: float32 [4096, 1024], P('shard', 'width'), may hold values from -0.09375 to 0.09375
- second_value: float32 [4096, 1024], P('shard', 'width'), may hold values from -0.09375 to 0.09375
- norm_train: float32 [4096], P(('shard', 'width')), may hold values from 0.25 to 1.75
- norm_step: float32 [4096], P(('shard', 'width')), may hold values from -0.3 to 0.3
Outputs:
- serving_query: bfloat16 [4096, 4096], P(None, 'width')
- serving_key: bfloat16 [4096, 1024], P(None, 'width')
- serving_value: bfloat16 [4096, 1024], P(None, 'width')
- column_query: float32 [4096], P('width')
- column_key: float32 [1024], P('width')
- column_value: float32 [1024], P('width')
- serve_norm: bfloat16 [4096], replicated
- whole_query: float32 [4096, 4096], P('shard', 'width')
- whole_key: float32 [4096, 1024], P('shard', 'width')
- whole_value: float32 [4096, 1024], P('shard', 'width')
All inputs are finite; a program needn't handle non-finite values. Where the computation divides by a largest or mean magnitude, that divisor is 1e-20 or more.
Results may differ from a plain program's by a relative error of at most 0.0004.
Values may be sent and summed in bfloat16 or wider, within the bound.
A program may use at most 128 MiB of HBM per device.

v0:
```python
import jax
import jax.numpy as jnp
from jax import lax
from jax.sharding import Mesh
from jax.sharding import PartitionSpec as P

D_MODEL = 4096
SHARD = ("shard_0", "shard_1", "shard_2")
SHARD_WIDTH = ("shard_0", "shard_1", "shard_2", "width")


learn_rate = 0.2
hold_rate = 0.8


def sent_to_all(shard, axis):
    count = lax.axis_size(axis)
    return lax.all_to_all(
        jnp.broadcast_to(shard[None], (count, *shard.shape)), axis, 0, 0, tiled=True
    )


def taken_together(shard, axis):
    everything = sent_to_all(shard, axis)
    return jnp.sum(everything, axis=0)


def together(arrays, axis):
    line, at, outs = (jnp.concatenate([a.reshape(-1) for a in arrays]), 0, [])
    running = taken_together(line, axis)
    for a in arrays:
        outs.append(running[at : at + a.size].reshape(a.shape))
        at += a.size
    return tuple(outs)


def side_by_side(arrays, axis, dim, along):
    ends, at = ([], 0)
    for a in arrays[:-1]:
        at += a.shape[along]
        ends.append(at)
    both = jnp.concatenate(arrays, axis=along)
    return tuple(jnp.split(lax.all_gather(both, axis, axis=dim, tiled=True), ends, axis=along))


def in_order(parts, dim):
    dims = list(parts.shape[1:])
    dims[dim] *= parts.shape[0]
    return jnp.moveaxis(parts, 0, dim).reshape(dims)


def stacked_from(shard, axes, order):
    parts = shard[None]
    for k in order:
        parts = lax.all_gather(parts, axes[k], axis=0, tiled=True)
    current = [lax.axis_size(axes[k]) for k in reversed(order)]
    parts = parts.reshape(*current, *shard.shape)
    turned = sorted(range(len(order)), key=lambda place: order[len(order) - 1 - place])
    return parts.transpose(*turned, *range(len(order), parts.ndim)).reshape(-1, *shard.shape)


def gather_axes(shard, axes, order, dim):
    return in_order(stacked_from(shard, axes, order), dim)


def local(
    w_query,
    first_query,
    second_query,
    w_key,
    first_key,
    second_key,
    w_value,
    first_value,
    second_value,
    norm_train,
    norm_step,
):
    hold_query = hold_rate * first_query + second_query
    whole_query = w_query - learn_rate * hold_query
    hold_key = hold_rate * first_key + second_key
    whole_key = w_key - learn_rate * hold_key
    hold_value = hold_rate * first_value + second_value
    whole_value = w_value - learn_rate * hold_value
    total_query, total_key, total_value = together(
        (
            jnp.sum(jnp.abs(whole_query), axis=0),
            jnp.sum(jnp.abs(whole_key), axis=0),
            jnp.sum(jnp.abs(whole_value), axis=0),
        ),
        SHARD,
    )
    column_query = total_query / D_MODEL
    column_key = total_key / D_MODEL
    column_value = total_value / D_MODEL
    narrow_query, narrow_key, narrow_value = (
        (whole_query / column_query).astype(jnp.bfloat16),
        (whole_key / column_key).astype(jnp.bfloat16),
        (whole_value / column_value).astype(jnp.bfloat16),
    )
    serving_query, serving_key, serving_value = side_by_side(
        (narrow_query, narrow_key, narrow_value), SHARD, 0, 1
    )
    serve_norm = gather_axes(
        (norm_train + norm_step).astype(jnp.bfloat16), SHARD_WIDTH, (0, 1, 3, 2), 0
    )
    return (
        serving_query,
        serving_key,
        serving_value,
        column_query,
        column_key,
        column_value,
        serve_norm,
        whole_query,
        whole_key,
        whole_value,
    )


def solution(mesh):
    split = Mesh(
        mesh.devices.reshape(8, 4, 2, mesh.shape["width"]),
        ("shard_0", "shard_1", "shard_2", "width"),
    )
    return jax.shard_map(
        local,
        mesh=split,
        in_specs=(
            P(SHARD, "width"),
            P(SHARD, "width"),
            P(SHARD, "width"),
            P(SHARD, "width"),
            P(SHARD, "width"),
            P(SHARD, "width"),
            P(SHARD, "width"),
            P(SHARD, "width"),
            P(SHARD, "width"),
            P(SHARD_WIDTH),
            P(SHARD_WIDTH),
        ),
        out_specs=(
            P(None, "width"),
            P(None, "width"),
            P(None, "width"),
            P("width"),
            P("width"),
            P("width"),
            P(),
            P(SHARD, "width"),
            P(SHARD, "width"),
            P(SHARD, "width"),
        ),
        check_vma=False,
    )
```

profile of v0, /device:TPU:1, one launch (start us, length us, event | category | flops | bytes accessed | tf_op | source)
XLA Modules:
  0.0 144.4 jit_solution(12513675102203945467)
XLA Ops:
  7.2 0.0 copy-start.8
  7.2 0.0 all-gather.4.cloned.1.call-start
  7.3 1.2 abs_reduce_fusion
  8.5 1.1 abs_reduce_fusion.1
  9.6 0.0 copy-start.2
  9.6 0.2 broadcast_in_dim.4
  9.8 27.9 %all_to_all.6 = f32[64,1,1536]{2,1,0:T(1,128)S(1)} all-to-all(f32[64,1,1536]{2,1,0:T(1,128)S(1)} %broadcast_in_dim.4), channel_id=1, replica_groups=mesh['shard_0'=8,'shard_1'=4,'shard_2'=2,'width'=4] {'shard_0','shard_1'..., dimensions={0} | all-to-all | bytes 786432 | tf_op jit(solution)/shard_map/all_to_all | solution.py:18
  37.8 0.2 reduce_sum.39
  38.1 0.0 copy-start.5
  38.2 0.7 pad_maximum_fusion
  38.9 0.0 all-gather.4.cloned.1.call-update
  38.9 0.6 dynamic-slice
  40.2 0.2 dynamic-update-slice
  40.4 12.6 %all-reduce = bf16[128]{0:T(256)(128)(2,1)S(1)} all-reduce(bf16[128]{0:T(256)(128)(2,1)S(1)} %dynamic-update-slice), channel_id=2, replica_groups=mesh['shard_0'=8,'shard_1'=4,'shard_2'=2,'width'=4] {'shard_0'}, use_global_device_ids=true, to_apply=%add | all-reduce | flops 128 | bytes 512
  53.1 0.1 reshape.33
  53.2 8.5 %all_gather.17 = bf16[32,16]{1,0:T(8,128)(2,1)S(1)} all-gather(bf16[8,16]{1,0:T(8,128)(2,1)S(1)} %reshape.33), channel_id=1, replica_groups=mesh['shard_0'=8,'shard_1'=4,'shard_2'=2,'width'=4] {'shard_1'}, dimensions={0}, use_global_device_ids=true | all-gather | bytes 1280 | tf_op jit(solution)/shard_map/all_gather | solution.py:55
  61.6 0.1 copy.29
  61.7 10.2 %all-gather.1 = bf16[4,32,16]{1,2,0:T(8,128)(2,1)S(1)} all-gather(bf16[1,32,16]{1,2,0:T(8,128)(2,1)S(1)} %copy.29), channel_id=1, replica_groups=mesh['shard_0'=8,'shard_1'=4,'shard_2'=2,'width'=4] {'width'}, dimensions={0}, use_global_device_ids=true | all-gather | bytes 5120 | tf_op jit(solution)/shard_map/all_gather | solution.py:55
  71.9 0.1 copy.30
  72.0 9.2 %all_gather.19 = bf16[256,16]{1,0:T(8,128)(2,1)S(1)} all-gather(bf16[128,16]{1,0:T(8,128)(2,1)S(1)} %bitcast.7), channel_id=1, replica_groups=mesh['shard_0'=8,'shard_1'=4,'shard_2'=2,'width'=4] {'shard_2'}, dimensions={0}, use_global_device_ids=true | all-gather | bytes 12288 | tf_op jit(solution)/shard_map/all_gather | solution.py:55
  81.3 0.7 reshape_reshape.3
  82.0 43.3 %all-gather.4.cloned.1.call-done = bf16[4096,1536]{1,0:T(8,128)(2,1)} async-done(((bf16[64,1536]{1,0:T(8,128)(2,1)}), bf16[4096,1536]{1,0:T(8,128)(2,1)}) %all-gather.4.cloned.1.call-update) | async-done | bytes 12582928 | tf_op jit(solution)/shard_map/all_gather | solution.py:43
  125.2 4.5 %fusion = (bf16[4096,256]{1,0:T(8,128)(2,1)}, bf16[4096,256]{1,0:T(8,128)(2,1)}) fusion(bf16[4096,1536]{1,0:T(8,128)(2,1)} %all-gather.4.cloned.1.call-done), kind=kLoop, calls=%fused_computation.15 | loop fusion | bytes 8388608 | tf_op jit(solution)/shard_map/split | solution.py:43
  129.8 7.8 %split.12 = bf16[4096,1024]{1,0:T(8,128)(2,1)} slice(bf16[4096,1536]{1,0:T(8,128)(2,1)} %all-gather.4.cloned.1.call-done), slice={[0:4096], [0:1024]} | slice | bytes 16777216 | tf_op jit(solution)/shard_map/split | solution.py:43
  (24 shorter events, 0.2 us)
Async XLA Ops:
  7.2 31.7 %copy-start.8 = (u32[256]{0:T(256)S(1)}, u32[256]{0:T(256)}, u32[]{:S(2)}) copy-start(u32[256]{0:T(256)} %constant.18) | copy-start | bytes 3076
  7.2 32.9 %copy-start.6 = (f32[16]{0:T(128)S(1)}, f32[16]{0:T(128)}, u32[]{:S(2)}) copy-start(f32[16]{0:T(128)} %param.20) | copy-start | bytes 196
  7.2 32.9 %copy-start.7 = (f32[16]{0:T(128)S(1)}, f32[16]{0:T(128)}, u32[]{:S(2)}) copy-start(f32[16]{0:T(128)} %param.21) | copy-start | bytes 196
  7.2 118.0 %all-gather.4.cloned.1.call-start = ((), (), s32[]{:S(2)}) async-start(), calls=%async_computation.1 | async-start | bytes 12779520 | tf_op jit(solution)/shard_map/all_gather | solution.py:43
  8.4 121.3 %copy-start = (f32[64,1024]{1,0:T(8,128)}, f32[64,1024]{1,0:T(8,128)S(1)}, u32[]{:S(2)}) copy-start(f32[64,1024]{1,0:T(8,128)S(1)} %get-tuple-element.11) | copy-start | bytes 786436
  9.6 120.1 %copy-start.1 = (f32[64,256]{1,0:T(8,128)}, f32[64,256]{1,0:T(8,128)S(1)}, u32[]{:S(2)}) copy-start(f32[64,256]{1,0:T(8,128)S(1)} %get-tuple-element.15) | copy-start | bytes 196612
  9.6 120.1 %copy-start.2 = (f32[64,256]{1,0:T(8,128)}, f32[64,256]{1,0:T(8,128)S(1)}, u32[]{:S(2)}) copy-start(f32[64,256]{1,0:T(8,128)S(1)} %get-tuple-element.21) | copy-start | bytes 196612
  38.0 91.7 %copy-start.4 = (f32[256]{0:T(256)}, f32[256]{0:T(256)S(1)}, u32[]{:S(2)}) copy-start(f32[256]{0:T(256)S(1)} %get-tuple-element.18) | copy-start | bytes 3076
  38.1 91.7 %copy-start.5 = (f32[256]{0:T(256)}, f32[256]{0:T(256)S(1)}, u32[]{:S(2)}) copy-start(f32[256]{0:T(256)S(1)} %get-tuple-element.19) | copy-start | bytes 3076
  38.1 91.7 %copy-start.3 = (f32[1024]{0:T(1024)}, f32[1024]{0:T(1024)S(1)}, u32[]{:S(2)}) copy-start(f32[1024]{0:T(1024)S(1)} %slice_multiply_fusion) | copy-start | bytes 12292
Sparse Core Ops, SparseCore 0:
  39.0 86.1 all-gather.3
where the time goes:
time: 145 us; the launch traced here: 144 us
  blocking collectives  68.5 us (47%)
  waiting for transfers between devices  43.3 us (30%)
  between operations  14.9 us (10%)
  local copies, waits for them, and re-layouts  14.4 us (10%)
  other arithmetic  3.35 us (2%)
    all_gather x1, waiting for transfers between devices, side_by_side(): lax.all_gather(both, axis, axis=dim, tiled=True)  43.3 us
    all_to_all x1, blocking collectives, sent_to_all(): lax.all_to_all(jnp.broadcast_to(shard[None], (count, *shard.shape)), axis...  27.9 us
    all_gather x3, blocking collectives, stacked_from(): parts = lax.all_gather(parts, axes[k], axis=0, tiled=True)  27.9 us
    unnamed x1, blocking collectives  12.6 us
    split x2, local copies, waits for them, and re-layouts, side_by_side(): jnp.split(lax.all_gather(both, axis, axis=dim, tiled=True), ends, axis=al...  12.3 us
  transfers between devices with their start and end apart: 1, of which 1 were waited for; matrix products, arithmetic and copies ran while one was open for 1% of the time, Pallas kernels for 0%

commit v1 on v0

v1 whole, which is shorter than its diff:
```python
import heapq

import jax
import jax.numpy as jnp
from jax import lax
from jax.experimental import pallas as pl
from jax.experimental.pallas import tpu as pltpu
from jax.sharding import PartitionSpec as P

D_MODEL = 4096
LEARN_RATE = 0.2
HOLD_RATE = 0.8
MESH = pl.DeviceIdType.MESH

NZ, NX, NC, NW = 8, 4, 2, 4
ROWS = D_MODEL // (NZ * NX * NC)
LANES = 128

PIECES = {
    "A0": (0, 0, 24),
    "A1": (0, 24, 16),
    "B0": (0, 40, 24),
    "B1": (1, 0, 64),
    "B2": (2, 0, 64),
}
BYTES = {"A0": 48, "A1": 32, "B0": 48, "B1": 32, "B2": 32}
STEP = {"+x": (1, 0), "-x": (-1, 0), "+z": (0, 1), "-z": (0, -1)}


def onward(message):
    colour, dx, dz, piece = message
    first = piece in ("A0", "B0")
    out = []

    def along(name, place, farthest, even):
        if place == 0:
            out.extend([("+" + name, 1), ("-" + name, -1)])
        elif 0 < place < farthest - 1 or (place == farthest - 1 and first == even):
            out.append(("+" + name, place + 1))
        elif -farthest + 1 < place < 0:
            out.append(("-" + name, place - 1))
        elif place == -farthest + 1 and first != even:
            out.append(("-" + name, farthest))

    if colour == "A":
        if dz == 0:
            along("x", dx, NX // 2, True)
            out = [(way, (colour, to, 0, piece)) for way, to in out]
            out += [("+z", (colour, dx, 1, piece)), ("-z", (colour, dx, -1, piece))]
        else:
            along("z", dz, NZ // 2, dx % 2 == 0)
            out = [(way, (colour, dx, to, piece)) for way, to in out]
    else:
        if dx == 0:
            along("z", dz, NZ // 2, True)
            out = [(way, (colour, 0, to, piece)) for way, to in out]
            out += [("+x", (colour, 1, dz, piece)), ("-x", (colour, -1, dz, piece))]
        else:
            along("x", dx, NX // 2, dz % 2 == 0)
            out = [(way, (colour, to, dz, piece)) for way, to in out]
    return out


def plan():
    rate, latency, step = 46.65e3 / 1024, 2.0, 0.05
    free = dict.fromkeys(STEP, 0.0)
    events, first = [], []

    def issue(now, way, message):
        free[way] = max(now, free[way]) + BYTES[message[3]] / rate
        heapq.heappush(events, (free[way] + latency, message))

    for axis, pieces in (("z", ("B0", "B1", "B2", "A0", "A1")), ("x", ("A0", "A1", "B0", "B1", "B2"))):
        for piece in pieces:
            for way, message in onward((piece[0], 0, 0, piece)):
                if way[1] == axis:
                    issue(0.0, way, message)
                    first.append((way, message))
    now, order = 0.0, []
    while events:
        at, message = heapq.heappop(events)
        now = max(now, at) + step
        order.append(message)
        for way, new in onward(message):
            issue(now, way, new)
    return first, order


FIRST, ORDER = plan()
INDEX = {message: i for i, message in enumerate(ORDER)}
SENT = dict.fromkeys(STEP, 0)
for _way, _message in FIRST:
    SENT[_way] += BYTES[_message[3]] // 16
for _message in ORDER:
    for _way, _new in onward(_message):
        SENT[_way] += BYTES[_new[3]] // 16


def gather_kernel(
    wq, fq, sq, wk, fk, sk, wv, fv, sv, nt, ns,
    oq, ok, ov, hq, hk, hv, cq, ck, cv, on,
    vq, vk, vv, vn, place, ring_n, ring_m, flat_n, part, line,
    load_sem, part_send, part_recv, line_send, line_recv, norm_send, norm_recv,
    send_sem, recv_sem, pair_send, pair_recv,
):
    shard = lax.axis_index("shard")
    width = lax.axis_index("width")
    core = lax.rem(shard, NC)
    chip = lax.div(shard, NC)
    x = lax.rem(chip, NX)
    z = lax.div(chip, NX)
    other = 1 - core

    def device(zz, xx, cc):
        return (zz * NX + xx) * NC + cc

    xs = [x] + [lax.rem(x + i, NX) for i in range(1, NX)]
    zs = [z] + [lax.rem(z + i, NZ) for i in range(1, NZ)]

    loads = []
    for i, (src, dst) in enumerate(((nt, vn.at[0]), (ns, vn.at[1]))):
        loads.append(pltpu.make_async_copy(src, dst, load_sem.at[9 + i]))
    for i, src in enumerate((wq, fq, sq, wk, fk, sk, wv, fv, sv)):
        dst = (vq, vk, vv)[i // 3].at[i % 3]
        loads.append(pltpu.make_async_copy(src, dst, load_sem.at[i]))
    for load in loads:
        load.start()

    x_peers = [(device(z, x, other), width)]
    x_peers += [(device(z, xs[i], c), width) for i in range(1, NX) for c in (core, other)]
    z_peers = [(device(zs[i], x, core), width) for i in range(1, NZ)]
    w_peers = [(device(z, x, c), lax.rem(width + i, NW)) for i in range(1, NW) for c in (core, other)]
    barrier = pltpu.get_barrier_semaphore()
    greeted = z_peers + x_peers + w_peers
    for peer in greeted:
        pl.semaphore_signal(barrier, 1, device_id=peer, device_id_type=MESH)

    def send(src, dst, send_to, recv_at, peer):
        copy = pltpu.make_async_remote_copy(
            src_ref=src, dst_ref=dst, send_sem=send_to, recv_sem=recv_at, device_id=peer, device_id_type=MESH
        )
        copy.start()

    def await_bytes(ref, sem):
        pltpu.make_async_copy(ref, ref, sem).wait()

    seat = core * NW + width
    for load in loads[:2]:
        load.wait()
    gain = (vn[0] + vn[1]).astype(jnp.bfloat16).astype(jnp.float32)
    place[...] = jnp.zeros_like(place)
    each = LANES // (NC * NW)
    for i in range(NC * NW):
        place[i : i + 1, i * each : (i + 1) * each] = gain
    ring_n[seat] = place[pl.ds(seat, 1), :]

    group = x * NC + core
    row = 0
    for n, (v, h) in enumerate(((vq, hq), (vk, hk), (vv, hv))):
        for load in loads[2 + 3 * n : 5 + 3 * n]:
            load.wait()
        for j in range(h.shape[1] // LANES):
            at = slice(j * LANES, (j + 1) * LANES)
            hold = HOLD_RATE * v[1, :, at] + v[2, :, at]
            whole = v[0, :, at] - LEARN_RATE * hold
            h[:, at] = whole
            part[group, row : row + 1, :] = jnp.sum(jnp.abs(whole), axis=0, keepdims=True)
            row += 1

    pl.semaphore_wait(barrier, len(greeted))

    for peer in x_peers:
        send(part.at[group], part.at[group], part_send, part_recv, peer)
    for peer in [x_peers[0]] + w_peers:
        send(ring_n.at[seat], ring_n.at[seat], norm_send.at[0], norm_recv.at[0], peer)
    await_bytes(part.at[pl.ds(0, 7)], part_recv)
    total = part[0]
    for i in range(1, NX * NC):
        total = total + part[i]
    line[z] = total
    for peer in z_peers:
        send(line.at[z], line.at[z], line_send, line_recv, peer)

    await_bytes(ring_n.at[pl.ds(0, 7)], norm_recv.at[0])
    gain = ring_n[0]
    for i in range(1, NC * NW):
        gain = gain + ring_n[i]
    ring_m[z, x] = gain
    for i in range(1, NX):
        send(ring_m.at[z, x], ring_m.at[z, x], norm_send.at[1], norm_recv.at[1], (device(z, xs[i], core), width))
    await_bytes(ring_m.at[0, pl.ds(0, 3)], norm_recv.at[1])
    for peer in z_peers:
        send(ring_m.at[z], ring_m.at[z], norm_send.at[2], norm_recv.at[2], peer)

    await_bytes(line.at[pl.ds(0, 7)], line_recv)
    total = line[0]
    for i in range(1, NZ):
        total = total + line[i]
    column = total * (1.0 / D_MODEL)
    cq[...] = column[0:8]
    ck[...] = column[8:10]
    cv[...] = column[10:12]
    scale = 1.0 / column
    row = 0
    for h, o in ((hq, oq), (hk, ok), (hv, ov)):
        for j in range(h.shape[1] // LANES):
            at = slice(j * LANES, (j + 1) * LANES)
            o[chip, core, :, at] = (h[:, at] * scale[row : row + 1, :]).astype(jnp.bfloat16)
            row += 1

    outs = (oq, ok, ov)
    peers = {
        "+x": (device(z, xs[1], core), width),
        "-x": (device(z, xs[NX - 1], core), width),
        "+z": (device(zs[1], x, core), width),
        "-z": (device(zs[NZ - 1], x, core), width),
    }
    pair = (device(z, x, other), width)
    ways = list(STEP)

    def block(dx, dz):
        return zs[-dz % NZ] * NX + xs[-dx % NX]

    def piece_ref(dx, dz, piece):
        array, start, rows = PIECES[piece]
        return outs[array].at[block(dx, dz), core, pl.ds(start, rows)]

    def forward(way, message):
        _, dx, dz, piece = message
        ref = piece_ref(dx - STEP[way][0], dz - STEP[way][1], piece)
        send(ref, ref, send_sem.at[ways.index(way)], recv_sem.at[INDEX[message]], peers[way])

    def across(dx, dz, piece):
        ref = piece_ref(dx, dz, piece)
        array = PIECES[piece][0]
        send(ref, ref, pair_send.at[array], pair_recv.at[array], pair)

    for way, message in FIRST:
        forward(way, message)
    for piece in PIECES:
        across(0, 0, piece)
    for message in ORDER:
        _, dx, dz, piece = message
        await_bytes(piece_ref(dx, dz, piece), recv_sem.at[INDEX[message]])
        for way, new in onward(message):
            forward(way, new)
        across(dx, dz, piece)

    await_bytes(ring_m.at[pl.ds(0, 7)], norm_recv.at[2])
    for i in range(NZ * NX):
        flat_n[i : i + 1, :] = ring_m[i // NX, i % NX]
    on[...] = flat_n[...].astype(jnp.bfloat16)

    for i, out in enumerate(outs):
        await_bytes(out.at[:, other], pair_recv.at[i])
        await_bytes(out.at[:, core], pair_send.at[i])
    for i, way in enumerate(ways):
        blocks, rest = divmod(SENT[way] * 8, ROWS)
        await_bytes(oq.at[pl.ds(0, blocks), 0], send_sem.at[i])
        if rest:
            await_bytes(oq.at[0, 0, pl.ds(0, rest)], send_sem.at[i])
    await_bytes(part.at[pl.ds(0, 7)], part_send)
    await_bytes(line.at[pl.ds(0, 7)], line_send)
    await_bytes(ring_n.at[pl.ds(0, 7)], norm_send.at[0])
    await_bytes(ring_m.at[0, pl.ds(0, 3)], norm_send.at[1])
    await_bytes(ring_m.at[pl.ds(0, 7)], norm_send.at[2])


def write_kernel(*refs):
    count = (len(refs) - 1) // 2
    copies = [pltpu.make_async_copy(refs[i], refs[count + i], refs[-1].at[i]) for i in range(count)]
    for copy in copies:
        copy.start()
    for copy in copies:
        copy.wait()


def local(wq, fq, sq, wk, fk, sk, wv, fv, sv, nt, ns):
    q, k, v = wq.shape[1], wk.shape[1], wv.shape[1]
    cols = (q, k, v)
    tiles = sum(cols) // LANES
    f32, bf16 = jnp.float32, jnp.bfloat16
    shapes = [((NZ * NX, NC, ROWS, n), bf16) for n in cols]
    shapes += [((ROWS, n), f32) for n in cols]
    shapes += [((n // LANES, LANES), f32) for n in cols]
    shapes += [((NZ * NX, LANES), bf16)]
    args = (wq, fq, sq, wk, fk, sk, wv, fv, sv, nt.reshape(1, -1), ns.reshape(1, -1))
    gathered = pl.pallas_call(
        gather_kernel,
        out_shape=[pltpu.VMEM(*s) for s in shapes],
        in_specs=[pl.BlockSpec(memory_space=pltpu.HBM)] * 11,
        out_specs=[pl.BlockSpec(memory_space=pltpu.VMEM)] * len(shapes),
        scratch_shapes=[
            pltpu.VMEM((3, ROWS, q), f32),
            pltpu.VMEM((3, ROWS, k), f32),
            pltpu.VMEM((3, ROWS, v), f32),
            pltpu.VMEM((2, 1, LANES // (NC * NW)), f32),
            pltpu.VMEM((NC * NW, LANES), f32),
            pltpu.VMEM((NC * NW, 1, LANES), f32),
            pltpu.VMEM((NZ, NX, 1, LANES), f32),
            pltpu.VMEM((NZ * NX, LANES), f32),
            pltpu.VMEM((NX * NC, tiles, LANES), f32),
            pltpu.VMEM((NZ, tiles, LANES), f32),
            pltpu.SemaphoreType.DMA((11,)),
            pltpu.SemaphoreType.DMA,
            pltpu.SemaphoreType.DMA,
            pltpu.SemaphoreType.DMA,
            pltpu.SemaphoreType.DMA,
            pltpu.SemaphoreType.DMA((3,)),
            pltpu.SemaphoreType.DMA((3,)),
            pltpu.SemaphoreType.DMA((4,)),
            pltpu.SemaphoreType.DMA((len(ORDER),)),
            pltpu.SemaphoreType.DMA((3,)),
            pltpu.SemaphoreType.DMA((3,)),
        ],
        compiler_params=pltpu.CompilerParams(
            collective_id=0, has_side_effects=True, vmem_limit_bytes=40 * 1024 * 1024
        ),
        name="update_sum_gather",
    )(*(pltpu.with_memory_space_constraint(a, pltpu.HBM) for a in args))
    written = pl.pallas_call(
        write_kernel,
        out_shape=[jax.ShapeDtypeStruct(*s) for s in shapes],
        in_specs=[pl.BlockSpec(memory_space=pltpu.VMEM)] * len(shapes),
        out_specs=[pl.BlockSpec(memory_space=pltpu.HBM)] * len(shapes),
        scratch_shapes=[pltpu.SemaphoreType.DMA((len(shapes),))],
        compiler_params=pltpu.CompilerParams(vmem_limit_bytes=1024 * 1024),
        name="write_outputs",
    )(*gathered)
    oq, ok, ov, hq, hk, hv, cq, ck, cv, on = written
    return (
        oq.reshape(D_MODEL, q),
        ok.reshape(D_MODEL, k),
        ov.reshape(D_MODEL, v),
        cq.reshape(q),
        ck.reshape(k),
        cv.reshape(v),
        on.reshape(D_MODEL),
        hq,
        hk,
        hv,
    )


def solution(mesh):
    block = P("shard", "width")
    spread = P(("shard", "width"))
    return jax.shard_map(
        local,
        mesh=mesh,
        in_specs=(block,) * 9 + (spread, spread),
        out_specs=(P(None, "width"),) * 3 + (P("width"),) * 3 + (P(),) + (block,) * 3,
        check_vma=False,
    )
```

time: 145 us -> 64.3 us (0.44)
  blocking collectives: 68.5 us -> 0 us
  Pallas kernels: 0 us -> 63.5 us
  waiting for transfers between devices: 43.3 us -> 0 us
  local copies, waits for them, and re-layouts: 14.4 us -> 0 us
  between operations: 14.9 us -> 0.65 us
  other arithmetic: 3.35 us -> 0 us
    pallas_call x0 -> x2, Pallas kernels: none -> 63.5 us  [the longest x1 58.7 us: local(): pl.pallas_call(gather_kernel, out_shape=[pltpu.VMEM(*s) for s in shapes],...]
    all_gather x1 -> x0, waiting for transfers between devices: 43.3 us -> none  [side_by_side(): lax.all_gather(both, axis, axis=dim, tiled=True)]
    all_to_all x1 -> x0, blocking collectives: 27.9 us -> none  [sent_to_all(): lax.all_to_all(jnp.broadcast_to(shard[None], (count, *shard.shape)), axis...]
    all_gather x3 -> x0, blocking collectives: 27.9 us -> none  [stacked_from(): parts = lax.all_gather(parts, axes[k], axis=0, tiled=True)]
    unnamed x1 -> x0, blocking collectives: 12.6 us -> none
    split x2 -> x0, local copies, waits for them, and re-layouts: 12.3 us -> none  [side_by_side(): jnp.split(lax.all_gather(both, axis, axis=dim, tiled=True), ends, axis=al...]
    reduce_sum x3 -> x0, other arithmetic: 2.58 us -> none  [the longest x1 1.18 us: local(): jnp.sum(jnp.abs(whole_query), axis=0)]
  transfers between devices with their start and end apart: 1 -> 0, of which waited for: 1 -> 0; matrix products, arithmetic and copies ran while one was open for 1% -> 0% of each run, Pallas kernels for 0% -> 0%
where the time goes in v1:
time: 64.3 us; the launch traced here: 64.2 us
  Pallas kernels  63.5 us (99%)
  between operations  0.65 us (1%)
    pallas_call x1, Pallas kernels, local(): pl.pallas_call(gather_kernel, out_shape=[pltpu.VMEM(*s) for s in shapes],...  58.7 us
    pallas_call x1, Pallas kernels, local(): pl.pallas_call(write_kernel, out_shape=[jax.ShapeDtypeStruct(*s) for s in...  4.85 us

profile of v1, /device:TPU:1, one launch (start us, length us, event | category | flops | bytes accessed | tf_op | source)
XLA Modules:
  0.0 64.2 jit_solution(15112525775063867947)
XLA Ops:
  0.6 58.7 %update_sum_gather.1 = (bf16[32,2,64,1024]{3,2,1,0:T(8,128)(2,1)S(1)}, bf16[32,2,64,256]{3,2,1,0:T(8,128)(2,1)S(1)}, bf16[32,2,64,256]{3,2,1,0:T(8,128)(2,1)S(1)...) custom-call(f32[64,1024]{1,0:T(8,128)} %wq.1, ...), custom_call_target="tpu_custom_call" | custom-call | tf_op jit(solution)/shard_map/update_sum_gather/pallas_call | solution.py:288
  59.3 4.9 %write_outputs.1 = (bf16[32,2,64,1024]{3,2,1,0:T(8,128)(2,1)}, bf16[32,2,64,256]{3,2,1,0:T(8,128)(2,1)}, bf16[32,2,64,256]{3,2,1,0:T(8,128)(2,1)}, f32[64,1024]{...) custom-call(bf16[32,2,64,1024]{3,2,1,0:T(8,128)(2,1)S(1)} %get-tuple, ...), custom_call_target="tpu_custom_call" | custom-call | tf_op jit(solution)/shard_map/write_outputs/pallas_call | solution.py:321

commit v2 on v1

--- a/solution.py
+++ b/solution.py
@@ -61,22 +61,40 @@
     return out
 
 
+EARLY_X = ("B0", "B1", "B2", "A0", "A1")
+EARLY_Z = (("B0", "B1"), ("A1", "A0"))
+EARLY = {"x": EARLY_X, "z": EARLY_Z[0] + EARLY_Z[1]}
+
+
+def own_hops(pieces, axis):
+    hops = [hop for piece in pieces for hop in onward((piece[0], 0, 0, piece))]
+    return [(way, message) for way, message in hops if way[1] == axis]
+
+
 def plan():
-    rate, latency, step = 46.65e3 / 1024, 2.0, 0.05
-    free = dict.fromkeys(STEP, 0.0)
-    events, first = [], []
-
-    def issue(now, way, message):
-        free[way] = max(now, free[way]) + BYTES[message[3]] / rate
+    rate, latency, step = 46.65e3 / 1024, 2.2, 0.05
+    stage_x, stage_z, taken_x, taken_z = 3.7, 4.8, 0.5, 1.05
+    free = {way: taken_x if way[1] == "x" else 0.0 for way in STEP}
+    events = []
+
+    def issue(now, way, message, width=1):
+        free[way] = max(now, free[way]) + width * BYTES[message[3]] / rate
         heapq.heappush(events, (free[way] + latency, message))
 
-    for axis, pieces in (("z", ("B0", "B1", "B2", "A0", "A1")), ("x", ("A0", "A1", "B0", "B1", "B2"))):
-        for piece in pieces:
-            for way, message in onward((piece[0], 0, 0, piece)):
-                if way[1] == axis:
-                    issue(0.0, way, message)
-                    first.append((way, message))
-    now, order = 0.0, []
+    for way, message in own_hops(EARLY_X, "x") + own_hops(EARLY_Z[0], "z"):
+        issue(0.0, way, message, 2)
+    start = max(stage_x, free["+z"])
+    for way in ("+z", "-z"):
+        free[way] = start + taken_z
+    for way, message in own_hops(EARLY_Z[1], "z"):
+        issue(start, way, message, 2)
+    start += stage_z + 0.2
+    events = [(max(at, start), message) for at, message in events]
+    heapq.heapify(events)
+    first = [hop for axis in "xz" for hop in own_hops([p for p in PIECES if p not in EARLY[axis]], axis)]
+    for way, message in first:
+        issue(start, way, message)
+    now, order = start, []
     while events:
         at, message = heapq.heappop(events)
         now = max(now, at) + step
@@ -88,6 +106,7 @@
 
 FIRST, ORDER = plan()
 INDEX = {message: i for i, message in enumerate(ORDER)}
+EARLY_WAY = {message: way for axis in "xz" for way, message in own_hops(EARLY[axis], axis)}
 SENT = dict.fromkeys(STEP, 0)
 for _way, _message in FIRST:
     SENT[_way] += BYTES[_message[3]] // 16
@@ -100,8 +119,8 @@
     wq, fq, sq, wk, fk, sk, wv, fv, sv, nt, ns,
     oq, ok, ov, hq, hk, hv, cq, ck, cv, on,
     vq, vk, vv, vn, place, ring_n, ring_m, flat_n, part, line,
-    load_sem, part_send, part_recv, line_send, line_recv, norm_send, norm_recv,
-    send_sem, recv_sem, pair_send, pair_recv,
+    scale, near_q, near_k, near_v, load_sem, part_send, part_recv, line_send, line_recv, norm_send, norm_recv,
+    early_send, send_sem, recv_sem, pair_send, pair_recv,
 ):
     shard = lax.axis_index("shard")
     width = lax.axis_index("width")
@@ -169,8 +188,30 @@
 
     pl.semaphore_wait(barrier, len(greeted))
 
+    ways = list(STEP)
+    peers = {
+        "+x": (device(z, xs[1], core), width),
+        "-x": (device(z, xs[NX - 1], core), width),
+        "+z": (device(zs[1], x, core), width),
+        "-z": (device(zs[NZ - 1], x, core), width),
+    }
+    wide = (hq, hk, hv)
+    near = (near_q, near_k, near_v)
+
+    def near_ref(way, piece):
+        array, start, rows = PIECES[piece]
+        return near[array].at[ways.index(way), pl.ds(start, rows)]
+
+    def early(pieces, axis):
+        for way, message in own_hops(pieces, axis):
+            array, start, rows = PIECES[message[3]]
+            src = wide[array].at[pl.ds(start, rows)]
+            send(src, near_ref(way, message[3]), early_send.at[ways.index(way)], recv_sem.at[INDEX[message]], peers[way])
+
     for peer in x_peers:
         send(part.at[group], part.at[group], part_send, part_recv, peer)
+    early(EARLY_X, "x")
+    early(EARLY_Z[0], "z")
     for peer in [x_peers[0]] + w_peers:
         send(ring_n.at[seat], ring_n.at[seat], norm_send.at[0], norm_recv.at[0], peer)
     await_bytes(part.at[pl.ds(0, 7)], part_recv)
@@ -180,17 +221,7 @@
     line[z] = total
     for peer in z_peers:
         send(line.at[z], line.at[z], line_send, line_recv, peer)
-
-    await_bytes(ring_n.at[pl.ds(0, 7)], norm_recv.at[0])
-    gain = ring_n[0]
-    for i in range(1, NC * NW):
-        gain = gain + ring_n[i]
-    ring_m[z, x] = gain
-    for i in range(1, NX):
-        send(ring_m.at[z, x], ring_m.at[z, x], norm_send.at[1], norm_recv.at[1], (device(z, xs[i], core), width))
-    await_bytes(ring_m.at[0, pl.ds(0, 3)], norm_recv.at[1])
-    for peer in z_peers:
-        send(ring_m.at[z], ring_m.at[z], norm_send.at[2], norm_recv.at[2], peer)
+    early(EARLY_Z[1], "z")
 
     await_bytes(line.at[pl.ds(0, 7)], line_recv)
     total = line[0]
@@ -200,23 +231,10 @@
     cq[...] = column[0:8]
     ck[...] = column[8:10]
     cv[...] = column[10:12]
-    scale = 1.0 / column
-    row = 0
-    for h, o in ((hq, oq), (hk, ok), (hv, ov)):
-        for j in range(h.shape[1] // LANES):
-            at = slice(j * LANES, (j + 1) * LANES)
-            o[chip, core, :, at] = (h[:, at] * scale[row : row + 1, :]).astype(jnp.bfloat16)
-            row += 1
+    scale[...] = 1.0 / column
 
     outs = (oq, ok, ov)
-    peers = {
-        "+x": (device(z, xs[1], core), width),
-        "-x": (device(z, xs[NX - 1], core), width),
-        "+z": (device(zs[1], x, core), width),
-        "-z": (device(zs[NZ - 1], x, core), width),
-    }
     pair = (device(z, x, other), width)
-    ways = list(STEP)
 
     def block(dx, dz):
         return zs[-dz % NZ] * NX + xs[-dx % NX]
@@ -235,16 +253,44 @@
         array = PIECES[piece][0]
         send(ref, ref, pair_send.at[array], pair_recv.at[array], pair)
 
+    def narrow(src, to, piece):
+        array, start, rows = PIECES[piece]
+        row = sum(h.shape[1] for h in wide[:array]) // LANES
+        for j in range(wide[array].shape[1] // LANES):
+            at = slice(j * LANES, (j + 1) * LANES)
+            part_of = src[:, at] * scale[row + j : row + j + 1, :]
+            outs[array][to, core, start : start + rows, at] = part_of.astype(jnp.bfloat16)
+
+    for piece, (array, start, rows) in PIECES.items():
+        narrow(wide[array].at[pl.ds(start, rows)], chip, piece)
     for way, message in FIRST:
         forward(way, message)
     for piece in PIECES:
         across(0, 0, piece)
-    for message in ORDER:
+    for step, message in enumerate(ORDER):
         _, dx, dz, piece = message
-        await_bytes(piece_ref(dx, dz, piece), recv_sem.at[INDEX[message]])
+        if message in EARLY_WAY:
+            src = near_ref(EARLY_WAY[message], piece)
+            await_bytes(src, recv_sem.at[step])
+            narrow(src, block(dx, dz), piece)
+        else:
+            await_bytes(piece_ref(dx, dz, piece), recv_sem.at[step])
         for way, new in onward(message):
             forward(way, new)
         across(dx, dz, piece)
+        if step == 40:
+            await_bytes(ring_n.at[pl.ds(0, 7)], norm_recv.at[0])
+            gain = ring_n[0]
+            for i in range(1, NC * NW):
+                gain = gain + ring_n[i]
+            ring_m[z, x] = gain
+            for i in range(1, NX):
+                peer = (device(z, xs[i], core), width)
+                send(ring_m.at[z, x], ring_m.at[z, x], norm_send.at[1], norm_recv.at[1], peer)
+        if step == 80:
+            await_bytes(ring_m.at[0, pl.ds(0, 3)], norm_recv.at[1])
+            for peer in z_peers:
+                send(ring_m.at[z], ring_m.at[z], norm_send.at[2], norm_recv.at[2], peer)
 
     await_bytes(ring_m.at[pl.ds(0, 7)], norm_recv.at[2])
     for i in range(NZ * NX):
@@ -259,6 +305,11 @@
         await_bytes(oq.at[pl.ds(0, blocks), 0], send_sem.at[i])
         if rest:
             await_bytes(oq.at[0, 0, pl.ds(0, rest)], send_sem.at[i])
+        whole, rest = divmod(sum(BYTES[p] for p in EARLY[way[1]]) // 2, ROWS)
+        for _ in range(whole):
+            await_bytes(hq, early_send.at[i])
+        if rest:
+            await_bytes(hq.at[pl.ds(0, rest)], early_send.at[i])
     await_bytes(part.at[pl.ds(0, 7)], part_send)
     await_bytes(line.at[pl.ds(0, 7)], line_send)
     await_bytes(ring_n.at[pl.ds(0, 7)], norm_send.at[0])
@@ -301,6 +352,10 @@
             pltpu.VMEM((NZ * NX, LANES), f32),
             pltpu.VMEM((NX * NC, tiles, LANES), f32),
             pltpu.VMEM((NZ, tiles, LANES), f32),
+            pltpu.VMEM((tiles, LANES), f32),
+            pltpu.VMEM((4, ROWS, q), f32),
+            pltpu.VMEM((4, ROWS, k), f32),
+            pltpu.VMEM((4, ROWS, v), f32),
             pltpu.SemaphoreType.DMA((11,)),
             pltpu.SemaphoreType.DMA,
             pltpu.SemaphoreType.DMA,
@@ -308,6 +363,7 @@
             pltpu.SemaphoreType.DMA,
             pltpu.SemaphoreType.DMA((3,)),
             pltpu.SemaphoreType.DMA((3,)),
+            pltpu.SemaphoreType.DMA((4,)),
             pltpu.SemaphoreType.DMA((4,)),
             pltpu.SemaphoreType.DMA((len(ORDER),)),
             pltpu.SemaphoreType.DMA((3,)),

time: 64.3 us -> 61.3 us (0.953)
  Pallas kernels: 63.5 us -> 60.5 us
    pallas_call x1, Pallas kernels: 58.7 us -> 55.7 us  [local(): pl.pallas_call(gather_kernel, out_shape=[pltpu.VMEM(*s) for s in shapes],...]
where the time goes in v2:
time: 61.3 us; the launch traced here: 61.2 us
  Pallas kernels  60.5 us (99%)
  between operations  0.65 us (1%)
    pallas_call x1, Pallas kernels, local(): pl.pallas_call(gather_kernel, out_shape=[pltpu.VMEM(*s) for s in shapes],...  55.7 us
    pallas_call x1, Pallas kernels, local(): pl.pallas_call(write_kernel, out_shape=[jax.ShapeDtypeStruct(*s) for s in...  4.85 us

profile of v2, /device:TPU:1, one launch (start us, length us, event | category | flops | bytes accessed | tf_op | source)
XLA Modules:
  0.0 61.2 jit_solution(6195581814738306725)
XLA Ops:
  0.6 55.7 %update_sum_gather.1 = (bf16[32,2,64,1024]{3,2,1,0:T(8,128)(2,1)S(1)}, bf16[32,2,64,256]{3,2,1,0:T(8,128)(2,1)S(1)}, bf16[32,2,64,256]{3,2,1,0:T(8,128)(2,1)S(1)...) custom-call(f32[64,1024]{1,0:T(8,128)} %wq.1, ...), custom_call_target="tpu_custom_call" | custom-call | tf_op jit(solution)/shard_map/update_sum_gather/pallas_call | solution.py:339
  56.3 4.9 %write_outputs.1 = (bf16[32,2,64,1024]{3,2,1,0:T(8,128)(2,1)}, bf16[32,2,64,256]{3,2,1,0:T(8,128)(2,1)}, bf16[32,2,64,256]{3,2,1,0:T(8,128)(2,1)}, f32[64,1024]{...) custom-call(bf16[32,2,64,1024]{3,2,1,0:T(8,128)(2,1)S(1)} %get-tuple, ...), custom_call_target="tpu_custom_call" | custom-call | tf_op jit(solution)/shard_map/write_outputs/pallas_call | solution.py:377

commit v3 on v2

--- a/solution.py
+++ b/solution.py
@@ -1,4 +1,5 @@
 import heapq
+import itertools
 
 import jax
 import jax.numpy as jnp
@@ -17,13 +18,14 @@
 LANES = 128
 
 PIECES = {
-    "A0": (0, 0, 24),
-    "A1": (0, 24, 16),
-    "B0": (0, 40, 24),
-    "B1": (1, 0, 64),
+    "A0": (0, 0, 16),
+    "A1": (0, 16, 16),
+    "A2": (1, 0, 24),
+    "B0": (0, 32, 32),
+    "B1": (1, 24, 40),
     "B2": (2, 0, 64),
 }
-BYTES = {"A0": 48, "A1": 32, "B0": 48, "B1": 32, "B2": 32}
+KIB = {"A0": 32, "A1": 32, "A2": 12, "B0": 64, "B1": 20, "B2": 32}
 STEP = {"+x": (1, 0), "-x": (-1, 0), "+z": (0, 1), "-z": (0, -1)}
 
 
@@ -61,8 +63,8 @@
     return out
 
 
-EARLY_X = ("B0", "B1", "B2", "A0", "A1")
-EARLY_Z = (("B0", "B1"), ("A1", "A0"))
+EARLY_X = ("A0", "A1", "A2", "B0", "B1", "B2")
+EARLY_Z = (("B0", "B1"), ("A0", "A1"))
 EARLY = {"x": EARLY_X, "z": EARLY_Z[0] + EARLY_Z[1]}
 
 
@@ -71,48 +73,64 @@
     return [(way, message) for way, message in hops if way[1] == axis]
 
 
+def hops_left(message):
+    hops, front = 0, [message]
+    while front := [new for old in front for _, new in onward(old)]:
+        hops += 1
+    return hops
+
+
 def plan():
-    rate, latency, step = 46.65e3 / 1024, 2.2, 0.05
+    rate, latency, step, slack = 46.65e3 / 1024, 2.2, 0.05, 2.0
     stage_x, stage_z, taken_x, taken_z = 3.7, 4.8, 0.5, 1.05
     free = {way: taken_x if way[1] == "x" else 0.0 for way in STEP}
-    events = []
-
-    def issue(now, way, message, width=1):
-        free[way] = max(now, free[way]) + width * BYTES[message[3]] / rate
+    waiting = {way: [] for way in STEP}
+    events, count = [], itertools.count()
+
+    def issue(now, way, message, width):
+        free[way] = max(now, free[way]) + width * KIB[message[3]] / rate
         heapq.heappush(events, (free[way] + latency, message))
+
+    def add(hops):
+        for way, message in hops:
+            heapq.heappush(waiting[way], (-hops_left(message), next(count), message))
+
+    def sends(now):
+        out = []
+        for way in STEP:
+            while waiting[way] and free[way] - now < slack:
+                message = heapq.heappop(waiting[way])[2]
+                issue(now, way, message, 1)
+                out.append((way, message))
+        return out
 
     for way, message in own_hops(EARLY_X, "x") + own_hops(EARLY_Z[0], "z"):
         issue(0.0, way, message, 2)
-    start = max(stage_x, free["+z"])
+    now = max(stage_x, free["+z"])
     for way in ("+z", "-z"):
-        free[way] = start + taken_z
+        free[way] = now + taken_z
     for way, message in own_hops(EARLY_Z[1], "z"):
-        issue(start, way, message, 2)
-    start += stage_z + 0.2
-    events = [(max(at, start), message) for at, message in events]
+        issue(now, way, message, 2)
+    now += stage_z + 0.2
+    events = [(max(at, now), message) for at, message in events]
     heapq.heapify(events)
-    first = [hop for axis in "xz" for hop in own_hops([p for p in PIECES if p not in EARLY[axis]], axis)]
-    for way, message in first:
-        issue(start, way, message)
-    now, order = start, []
+    for axis in "xz":
+        add(own_hops([p for p in PIECES if p not in EARLY[axis]], axis))
+    first, steps = sends(now), []
     while events:
         at, message = heapq.heappop(events)
         now = max(now, at) + step
-        order.append(message)
-        for way, new in onward(message):
-            issue(now, way, new)
-    return first, order
-
-
-FIRST, ORDER = plan()
-INDEX = {message: i for i, message in enumerate(ORDER)}
+        add(onward(message))
+        steps.append((message, sends(now)))
+    return first, steps
+
+
+FIRST, STEPS = plan()
+INDEX = {message: i for i, (message, _) in enumerate(STEPS)}
 EARLY_WAY = {message: way for axis in "xz" for way, message in own_hops(EARLY[axis], axis)}
 SENT = dict.fromkeys(STEP, 0)
-for _way, _message in FIRST:
-    SENT[_way] += BYTES[_message[3]] // 16
-for _message in ORDER:
-    for _way, _new in onward(_message):
-        SENT[_way] += BYTES[_new[3]] // 16
+for _way, _message in FIRST + [send for _, sends in STEPS for send in sends]:
+    SENT[_way] += KIB[_message[3]]
 
 
 def gather_kernel(
@@ -163,6 +181,17 @@
     def await_bytes(ref, sem):
         pltpu.make_async_copy(ref, ref, sem).wait()
 
+    def await_kib(kib, whole_q, rows_q, rows_k, sem):
+        count, kib = divmod(kib, 128)
+        if count:
+            await_bytes(whole_q(count), sem)
+        count, kib = divmod(kib, 16)
+        if count:
+            await_bytes(rows_q.at[pl.ds(0, 8 * count)], sem)
+        count = kib // 4
+        if count:
+            await_bytes(rows_k.at[pl.ds(0, 8 * count)], sem)
+
     seat = core * NW + width
     for load in loads[:2]:
         load.wait()
@@ -267,7 +296,7 @@
         forward(way, message)
     for piece in PIECES:
         across(0, 0, piece)
-    for step, message in enumerate(ORDER):
+    for step, (message, sends) in enumerate(STEPS):
         _, dx, dz, piece = message
         if message in EARLY_WAY:
             src = near_ref(EARLY_WAY[message], piece)
@@ -275,10 +304,10 @@
             narrow(src, block(dx, dz), piece)
         else:
             await_bytes(piece_ref(dx, dz, piece), recv_sem.at[step])
-        for way, new in onward(message):
+        for way, new in sends:
             forward(way, new)
         across(dx, dz, piece)
-        if step == 40:
+        if step == len(STEPS) // 4:
             await_bytes(ring_n.at[pl.ds(0, 7)], norm_recv.at[0])
             gain = ring_n[0]
             for i in range(1, NC * NW):
@@ -287,7 +316,7 @@
             for i in range(1, NX):
                 peer = (device(z, xs[i], core), width)
                 send(ring_m.at[z, x], ring_m.at[z, x], norm_send.at[1], norm_recv.at[1], peer)
-        if step == 80:
+        if step == len(STEPS) // 2:
             await_bytes(ring_m.at[0, pl.ds(0, 3)], norm_recv.at[1])
             for peer in z_peers:
                 send(ring_m.at[z], ring_m.at[z], norm_send.at[2], norm_recv.at[2], peer)
@@ -301,15 +330,8 @@
         await_bytes(out.at[:, other], pair_recv.at[i])
         await_bytes(out.at[:, core], pair_send.at[i])
     for i, way in enumerate(ways):
-        blocks, rest = divmod(SENT[way] * 8, ROWS)
-        await_bytes(oq.at[pl.ds(0, blocks), 0], send_sem.at[i])
-        if rest:
-            await_bytes(oq.at[0, 0, pl.ds(0, rest)], send_sem.at[i])
-        whole, rest = divmod(sum(BYTES[p] for p in EARLY[way[1]]) // 2, ROWS)
-        for _ in range(whole):
-            await_bytes(hq, early_send.at[i])
-        if rest:
-            await_bytes(hq.at[pl.ds(0, rest)], early_send.at[i])
+        await_kib(SENT[way], lambda n: oq.at[pl.ds(0, n), 0], oq.at[0, 0], ok.at[0, 0], send_sem.at[i])
+        await_kib(sum(KIB[p] for p in EARLY[way[1]]), lambda n: near_q.at[pl.ds(0, n)], hq, hk, early_send.at[i])
     await_bytes(part.at[pl.ds(0, 7)], part_send)
     await_bytes(line.at[pl.ds(0, 7)], line_send)
     await_bytes(ring_n.at[pl.ds(0, 7)], norm_send.at[0])
@@ -365,7 +387,7 @@
             pltpu.SemaphoreType.DMA((3,)),
             pltpu.SemaphoreType.DMA((4,)),
             pltpu.SemaphoreType.DMA((4,)),
-            pltpu.SemaphoreType.DMA((len(ORDER),)),
+            pltpu.SemaphoreType.DMA((len(STEPS),)),
             pltpu.SemaphoreType.DMA((3,)),
             pltpu.SemaphoreType.DMA((3,)),
         ],

time: 61.3 us -> 59.3 us (0.967)
  Pallas kernels: 60.5 us -> 58.5 us
    pallas_call x1, Pallas kernels: 55.7 us -> 53.7 us  [local(): pl.pallas_call(gather_kernel, out_shape=[pltpu.VMEM(*s) for s in shapes],...]
where the time goes in v3:
time: 59.3 us; the launch traced here: 59.2 us
  Pallas kernels  58.5 us (99%)
  between operations  0.65 us (1%)
    pallas_call x1, Pallas kernels, local(): pl.pallas_call(gather_kernel, out_shape=[pltpu.VMEM(*s) for s in shapes],...  53.7 us
    pallas_call x1, Pallas kernels, local(): pl.pallas_call(write_kernel, out_shape=[jax.ShapeDtypeStruct(*s) for s in...  4.85 us

profile of v3, /device:TPU:1, one launch (start us, length us, event | category | flops | bytes accessed | tf_op | source)
XLA Modules:
  0.0 59.2 jit_solution(1571543494164080899)
XLA Ops:
  0.6 53.7 %update_sum_gather.1 = (bf16[32,2,64,1024]{3,2,1,0:T(8,128)(2,1)S(1)}, bf16[32,2,64,256]{3,2,1,0:T(8,128)(2,1)S(1)}, bf16[32,2,64,256]{3,2,1,0:T(8,128)(2,1)S(1)...) custom-call(f32[64,1024]{1,0:T(8,128)} %wq.1, ...), custom_call_target="tpu_custom_call" | custom-call | tf_op jit(solution)/shard_map/update_sum_gather/pallas_call | solution.py:361
  54.3 4.9 %write_outputs.1 = (bf16[32,2,64,1024]{3,2,1,0:T(8,128)(2,1)}, bf16[32,2,64,256]{3,2,1,0:T(8,128)(2,1)}, bf16[32,2,64,256]{3,2,1,0:T(8,128)(2,1)}, f32[64,1024]{...) custom-call(bf16[32,2,64,1024]{3,2,1,0:T(8,128)(2,1)S(1)} %get-tuple, ...), custom_call_target="tpu_custom_call" | custom-call | tf_op jit(solution)/shard_map/write_outputs/pallas_call | solution.py:399

commit v4 on v3

--- a/solution.py
+++ b/solution.py
@@ -81,8 +81,8 @@
 
 
 def plan():
-    rate, latency, step, slack = 46.65e3 / 1024, 2.2, 0.05, 2.0
-    stage_x, stage_z, taken_x, taken_z = 3.7, 4.8, 0.5, 1.05
+    rate, latency, step, slack = 46.65e3 / 1024, 2.8, 0.05, 2.0
+    stage_x, stage_z, taken_x, taken_z = 4.5, 5.5, 0.5, 1.05
     free = {way: taken_x if way[1] == "x" else 0.0 for way in STEP}
     waiting = {way: [] for way in STEP}
     events, count = [], itertools.count()
@@ -163,9 +163,9 @@
     for load in loads:
         load.start()
 
-    x_peers = [(device(z, x, other), width)]
-    x_peers += [(device(z, xs[i], c), width) for i in range(1, NX) for c in (core, other)]
-    z_peers = [(device(zs[i], x, core), width) for i in range(1, NZ)]
+    x_peers = [(device(z, xs[i], c), width) for i in (2, 1, 3) for c in (other, core)]
+    x_peers += [(device(z, x, other), width)]
+    z_peers = [(device(zs[i], x, core), width) for i in (4, 3, 5, 2, 6, 1, 7)]
     w_peers = [(device(z, x, c), lax.rem(width + i, NW)) for i in range(1, NW) for c in (core, other)]
     barrier = pltpu.get_barrier_semaphore()
     greeted = z_peers + x_peers + w_peers
@@ -241,7 +241,7 @@
         send(part.at[group], part.at[group], part_send, part_recv, peer)
     early(EARLY_X, "x")
     early(EARLY_Z[0], "z")
-    for peer in [x_peers[0]] + w_peers:
+    for peer in [x_peers[-1]] + w_peers:
         send(ring_n.at[seat], ring_n.at[seat], norm_send.at[0], norm_recv.at[0], peer)
     await_bytes(part.at[pl.ds(0, 7)], part_recv)
     total = part[0]

time: 59.3 us -> 58.3 us (0.983)
  Pallas kernels: 58.5 us -> 57.5 us
    pallas_call x1, Pallas kernels: 53.7 us -> 52.7 us  [local(): pl.pallas_call(gather_kernel, out_shape=[pltpu.VMEM(*s) for s in shapes],...]
where the time goes in v4:
time: 58.3 us; the launch traced here: 58.2 us
  Pallas kernels  57.5 us (99%)
  between operations  0.65 us (1%)
    pallas_call x1, Pallas kernels, local(): pl.pallas_call(gather_kernel, out_shape=[pltpu.VMEM(*s) for s in shapes],...  52.7 us
    pallas_call x1, Pallas kernels, local(): pl.pallas_call(write_kernel, out_shape=[jax.ShapeDtypeStruct(*s) for s in...  4.85 us

profile of v4, /device:TPU:1, one launch (start us, length us, event | category | flops | bytes accessed | tf_op | source)
XLA Modules:
  0.0 58.2 jit_solution(8424836121140400057)
XLA Ops:
  0.6 52.7 %update_sum_gather.1 = (bf16[32,2,64,1024]{3,2,1,0:T(8,128)(2,1)S(1)}, bf16[32,2,64,256]{3,2,1,0:T(8,128)(2,1)S(1)}, bf16[32,2,64,256]{3,2,1,0:T(8,128)(2,1)S(1)...) custom-call(f32[64,1024]{1,0:T(8,128)} %wq.1, ...), custom_call_target="tpu_custom_call" | custom-call | tf_op jit(solution)/shard_map/update_sum_gather/pallas_call | solution.py:361
  53.3 4.9 %write_outputs.1 = (bf16[32,2,64,1024]{3,2,1,0:T(8,128)(2,1)}, bf16[32,2,64,256]{3,2,1,0:T(8,128)(2,1)}, bf16[32,2,64,256]{3,2,1,0:T(8,128)(2,1)}, f32[64,1024]{...) custom-call(bf16[32,2,64,1024]{3,2,1,0:T(8,128)(2,1)S(1)} %get-tuple, ...), custom_call_target="tpu_custom_call" | custom-call | tf_op jit(solution)/shard_map/write_outputs/pallas_call | solution.py:399

commit v5 on v4

--- a/solution.py
+++ b/solution.py
@@ -128,16 +128,39 @@
 FIRST, STEPS = plan()
 INDEX = {message: i for i, (message, _) in enumerate(STEPS)}
 EARLY_WAY = {message: way for axis in "xz" for way, message in own_hops(EARLY[axis], axis)}
-SENT = dict.fromkeys(STEP, 0)
-for _way, _message in FIRST + [send for _, sends in STEPS for send in sends]:
-    SENT[_way] += KIB[_message[3]]
+SENT = sum(KIB[message[3]] for _, message in FIRST + [hop for _, sends in STEPS for hop in sends])
+
+
+def slots():
+    turn = {"+x": "-x", "-x": "+x", "+z": "-z", "-z": "+z"}
+    sent = [(-1, way, message) for axis in "xz" for way, message in own_hops(EARLY[axis], axis)]
+    sent += [(-1, way, message) for way, message in FIRST]
+    sent += [(step, way, message) for step, (_, sends) in enumerate(STEPS) for way, message in sends]
+
+    def known(old, way):
+        later = [INDEX[m] for at, back, m in sent if back == turn[way] and at >= max(0, INDEX[old])]
+        return min(later, default=len(STEPS))
+
+    last, slot = [], {}
+    for at, way, message in sorted(sent, key=lambda entry: (entry[0], INDEX[entry[2]])):
+        free = [i for i, old in enumerate(last) if at >= 0 and known(old, way) <= at]
+        if free:
+            slot[message] = free[0]
+            last[free[0]] = message
+        else:
+            slot[message] = len(last)
+            last.append(message)
+    return slot
+
+
+SLOT = slots()
 
 
 def gather_kernel(
     wq, fq, sq, wk, fk, sk, wv, fv, sv, nt, ns,
     oq, ok, ov, hq, hk, hv, cq, ck, cv, on,
     vq, vk, vv, vn, place, ring_n, ring_m, flat_n, part, line,
-    scale, near_q, near_k, near_v, load_sem, part_send, part_recv, line_send, line_recv, norm_send, norm_recv,
+    scale, near_q, near_k, near_v, load_sem, part_recv, line_recv, norm_send, norm_recv,
     early_send, send_sem, recv_sem, pair_send, pair_recv,
 ):
     shard = lax.axis_index("shard")
@@ -156,10 +179,10 @@
 
     loads = []
     for i, (src, dst) in enumerate(((nt, vn.at[0]), (ns, vn.at[1]))):
-        loads.append(pltpu.make_async_copy(src, dst, load_sem.at[9 + i]))
+        loads.append(pltpu.make_async_copy(src, dst, load_sem.at[3 + i]))
     for i, src in enumerate((wq, fq, sq, wk, fk, sk, wv, fv, sv)):
         dst = (vq, vk, vv)[i // 3].at[i % 3]
-        loads.append(pltpu.make_async_copy(src, dst, load_sem.at[i]))
+        loads.append(pltpu.make_async_copy(src, dst, load_sem.at[i // 3]))
     for load in loads:
         load.start()
 
@@ -205,8 +228,7 @@
     group = x * NC + core
     row = 0
     for n, (v, h) in enumerate(((vq, hq), (vk, hk), (vv, hv))):
-        for load in loads[2 + 3 * n : 5 + 3 * n]:
-            load.wait()
+        await_bytes(v, load_sem.at[n])
         for j in range(h.shape[1] // LANES):
             at = slice(j * LANES, (j + 1) * LANES)
             hold = HOLD_RATE * v[1, :, at] + v[2, :, at]
@@ -235,21 +257,21 @@
         for way, message in own_hops(pieces, axis):
             array, start, rows = PIECES[message[3]]
             src = wide[array].at[pl.ds(start, rows)]
-            send(src, near_ref(way, message[3]), early_send.at[ways.index(way)], recv_sem.at[INDEX[message]], peers[way])
+            send(src, near_ref(way, message[3]), early_send, recv_sem.at[SLOT[message]], peers[way])
 
     for peer in x_peers:
-        send(part.at[group], part.at[group], part_send, part_recv, peer)
+        send(part.at[group], part.at[group], norm_send, part_recv, peer)
     early(EARLY_X, "x")
     early(EARLY_Z[0], "z")
     for peer in [x_peers[-1]] + w_peers:
-        send(ring_n.at[seat], ring_n.at[seat], norm_send.at[0], norm_recv.at[0], peer)
+        send(ring_n.at[seat], ring_n.at[seat], norm_send, norm_recv.at[0], peer)
     await_bytes(part.at[pl.ds(0, 7)], part_recv)
     total = part[0]
     for i in range(1, NX * NC):
         total = total + part[i]
     line[z] = total
     for peer in z_peers:
-        send(line.at[z], line.at[z], line_send, line_recv, peer)
+        send(line.at[z], line.at[z], norm_send, line_recv, peer)
     early(EARLY_Z[1], "z")
 
     await_bytes(line.at[pl.ds(0, 7)], line_recv)
@@ -275,7 +297,7 @@
     def forward(way, message):
         _, dx, dz, piece = message
         ref = piece_ref(dx - STEP[way][0], dz - STEP[way][1], piece)
-        send(ref, ref, send_sem.at[ways.index(way)], recv_sem.at[INDEX[message]], peers[way])
+        send(ref, ref, send_sem, recv_sem.at[SLOT[message]], peers[way])
 
     def across(dx, dz, piece):
         ref = piece_ref(dx, dz, piece)
@@ -300,10 +322,10 @@
         _, dx, dz, piece = message
         if message in EARLY_WAY:
             src = near_ref(EARLY_WAY[message], piece)
-            await_bytes(src, recv_sem.at[step])
+            await_bytes(src, recv_sem.at[SLOT[message]])
             narrow(src, block(dx, dz), piece)
         else:
-            await_bytes(piece_ref(dx, dz, piece), recv_sem.at[step])
+            await_bytes(piece_ref(dx, dz, piece), recv_sem.at[SLOT[message]])
         for way, new in sends:
             forward(way, new)
         across(dx, dz, piece)
@@ -315,11 +337,11 @@
             ring_m[z, x] = gain
             for i in range(1, NX):
                 peer = (device(z, xs[i], core), width)
-                send(ring_m.at[z, x], ring_m.at[z, x], norm_send.at[1], norm_recv.at[1], peer)
+                send(ring_m.at[z, x], ring_m.at[z, x], norm_send, norm_recv.at[1], peer)
         if step == len(STEPS) // 2:
             await_bytes(ring_m.at[0, pl.ds(0, 3)], norm_recv.at[1])
             for peer in z_peers:
-                send(ring_m.at[z], ring_m.at[z], norm_send.at[2], norm_recv.at[2], peer)
+                send(ring_m.at[z], ring_m.at[z], norm_send, norm_recv.at[2], peer)
 
     await_bytes(ring_m.at[pl.ds(0, 7)], norm_recv.at[2])
     for i in range(NZ * NX):
@@ -329,14 +351,17 @@
     for i, out in enumerate(outs):
         await_bytes(out.at[:, other], pair_recv.at[i])
         await_bytes(out.at[:, core], pair_send.at[i])
-    for i, way in enumerate(ways):
-        await_kib(SENT[way], lambda n: oq.at[pl.ds(0, n), 0], oq.at[0, 0], ok.at[0, 0], send_sem.at[i])
-        await_kib(sum(KIB[p] for p in EARLY[way[1]]), lambda n: near_q.at[pl.ds(0, n)], hq, hk, early_send.at[i])
-    await_bytes(part.at[pl.ds(0, 7)], part_send)
-    await_bytes(line.at[pl.ds(0, 7)], line_send)
-    await_bytes(ring_n.at[pl.ds(0, 7)], norm_send.at[0])
-    await_bytes(ring_m.at[0, pl.ds(0, 3)], norm_send.at[1])
-    await_bytes(ring_m.at[pl.ds(0, 7)], norm_send.at[2])
+    half = SENT // 8 * 4
+    for kib in (half, SENT - half):
+        await_kib(kib, lambda n: oq.at[pl.ds(0, n), 0], oq.at[0, 0], ok.at[0, 0], send_sem)
+    early_kib = 2 * sum(KIB[p] for axis in "xz" for p in EARLY[axis])
+    for _ in range(2):
+        await_kib(early_kib // 2, lambda n: near_q.at[pl.ds(0, n)], hq, hk, early_send)
+    await_bytes(part.at[pl.ds(0, 7)], norm_send)
+    await_bytes(line.at[pl.ds(0, 7)], norm_send)
+    await_bytes(ring_n.at[pl.ds(0, 7)], norm_send)
+    await_bytes(ring_m.at[0, pl.ds(0, 3)], norm_send)
+    await_bytes(ring_m.at[pl.ds(0, 7)], norm_send)
 
 
 def write_kernel(*refs):
@@ -378,16 +403,14 @@
             pltpu.VMEM((4, ROWS, q), f32),
             pltpu.VMEM((4, ROWS, k), f32),
             pltpu.VMEM((4, ROWS, v), f32),
-            pltpu.SemaphoreType.DMA((11,)),
-            pltpu.SemaphoreType.DMA,
+            pltpu.SemaphoreType.DMA((5,)),
             pltpu.SemaphoreType.DMA,
             pltpu.SemaphoreType.DMA,
             pltpu.SemaphoreType.DMA,
             pltpu.SemaphoreType.DMA((3,)),
-            pltpu.SemaphoreType.DMA((3,)),
-            pltpu.SemaphoreType.DMA((4,)),
-            pltpu.SemaphoreType.DMA((4,)),
-            pltpu.SemaphoreType.DMA((len(STEPS),)),
+            pltpu.SemaphoreType.DMA,
+            pltpu.SemaphoreType.DMA,
+            pltpu.SemaphoreType.DMA((1 + max(SLOT.values()),)),
             pltpu.SemaphoreType.DMA((3,)),
             pltpu.SemaphoreType.DMA((3,)),
         ],

time: 58.3 us -> 57.1 us (0.979)
  Pallas kernels: 57.5 us -> 56.3 us
    pallas_call x1, Pallas kernels: 52.7 us -> 51.5 us  [local(): pl.pallas_call(gather_kernel, out_shape=[pltpu.VMEM(*s) for s in shapes],...]
where the time goes in v5:
time: 57.1 us; the launch traced here: 57 us
  Pallas kernels  56.3 us (99%)
  between operations  0.65 us (1%)
    pallas_call x1, Pallas kernels, local(): pl.pallas_call(gather_kernel, out_shape=[pltpu.VMEM(*s) for s in shapes],...  51.5 us
    pallas_call x1, Pallas kernels, local(): pl.pallas_call(write_kernel, out_shape=[jax.ShapeDtypeStruct(*s) for s in...  4.85 us

profile of v5, /device:TPU:1, one launch (start us, length us, event | category | flops | bytes accessed | tf_op | source)
XLA Modules:
  0.0 57.0 jit_solution(4359777927048438251)
XLA Ops:
  0.6 51.5 %update_sum_gather.1 = (bf16[32,2,64,1024]{3,2,1,0:T(8,128)(2,1)S(1)}, bf16[32,2,64,256]{3,2,1,0:T(8,128)(2,1)S(1)}, bf16[32,2,64,256]{3,2,1,0:T(8,128)(2,1)S(1)...) custom-call(f32[64,1024]{1,0:T(8,128)} %wq.1, ...), custom_call_target="tpu_custom_call" | custom-call | tf_op jit(solution)/shard_map/update_sum_gather/pallas_call | solution.py:386
  52.1 4.9 %write_outputs.1 = (bf16[32,2,64,1024]{3,2,1,0:T(8,128)(2,1)}, bf16[32,2,64,256]{3,2,1,0:T(8,128)(2,1)}, bf16[32,2,64,256]{3,2,1,0:T(8,128)(2,1)}, f32[64,1024]{...) custom-call(bf16[32,2,64,1024]{3,2,1,0:T(8,128)(2,1)S(1)} %get-tuple, ...), custom_call_target="tpu_custom_call" | custom-call | tf_op jit(solution)/shard_map/write_outputs/pallas_call | solution.py:422

commit v6 on v5

--- a/solution.py
+++ b/solution.py
@@ -21,17 +21,18 @@
     "A0": (0, 0, 16),
     "A1": (0, 16, 16),
     "A2": (1, 0, 24),
-    "B0": (0, 32, 32),
+    "B0": (0, 32, 16),
+    "B3": (0, 48, 16),
     "B1": (1, 24, 40),
     "B2": (2, 0, 64),
 }
-KIB = {"A0": 32, "A1": 32, "A2": 12, "B0": 64, "B1": 20, "B2": 32}
+KIB = {"A0": 32, "A1": 32, "A2": 12, "B0": 32, "B3": 32, "B1": 20, "B2": 32}
 STEP = {"+x": (1, 0), "-x": (-1, 0), "+z": (0, 1), "-z": (0, -1)}
 
 
 def onward(message):
     colour, dx, dz, piece = message
-    first = piece in ("A0", "B0")
+    first = piece in ("A0", "B0", "B1")
     out = []
 
     def along(name, place, farthest, even):
@@ -63,8 +64,8 @@
     return out
 
 
-EARLY_X = ("A0", "A1", "A2", "B0", "B1", "B2")
-EARLY_Z = (("B0", "B1"), ("A0", "A1"))
+EARLY_X = ("A0", "A1", "A2", "B0", "B3", "B1", "B2")
+EARLY_Z = (("B0", "B3", "B1"), ("A0", "A1"))
 EARLY = {"x": EARLY_X, "z": EARLY_Z[0] + EARLY_Z[1]}
 
 

time: 57.1 us -> 57 us (level)
  no operation moved by 1% of the time
where the time goes in v6:
time: 57 us; the launch traced here: 56.9 us
  Pallas kernels  56.3 us (99%)
  between operations  0.65 us (1%)
    pallas_call x1, Pallas kernels, local(): pl.pallas_call(gather_kernel, out_shape=[pltpu.VMEM(*s) for s in shapes],...  51.4 us
    pallas_call x1, Pallas kernels, local(): pl.pallas_call(write_kernel, out_shape=[jax.ShapeDtypeStruct(*s) for s in...  4.85 us

profile of v6, /device:TPU:1, one launch (start us, length us, event | category | flops | bytes accessed | tf_op | source)
XLA Modules:
  0.0 56.9 jit_solution(405852734550881394)
XLA Ops:
  0.6 51.4 %update_sum_gather.1 = (bf16[32,2,64,1024]{3,2,1,0:T(8,128)(2,1)S(1)}, bf16[32,2,64,256]{3,2,1,0:T(8,128)(2,1)S(1)}, bf16[32,2,64,256]{3,2,1,0:T(8,128)(2,1)S(1)...) custom-call(f32[64,1024]{1,0:T(8,128)} %wq.1, ...), custom_call_target="tpu_custom_call" | custom-call | tf_op jit(solution)/shard_map/update_sum_gather/pallas_call | solution.py:387
  52.1 4.9 %write_outputs.1 = (bf16[32,2,64,1024]{3,2,1,0:T(8,128)(2,1)}, bf16[32,2,64,256]{3,2,1,0:T(8,128)(2,1)}, bf16[32,2,64,256]{3,2,1,0:T(8,128)(2,1)}, f32[64,1024]{...) custom-call(bf16[32,2,64,1024]{3,2,1,0:T(8,128)(2,1)S(1)} %get-tuple, ...), custom_call_target="tpu_custom_call" | custom-call | tf_op jit(solution)/shard_map/write_outputs/pallas_call | solution.py:423
